TPU v7x, 32 devices: a whole 2x2x4 slice. The times are simulated.
32 devices in a mesh: row: 4 (over z), col: 8 (over y, x, core).
Axes of the slice: x: 2, y: 2, z: 4, core: 2. Of those that a mesh axis runs over, the one named last changes fastest.
Arguments:
- front: float32 [12288, 12288], P('row', 'col'), as said below
- structure: int32 [3, 96], replicated, may hold values from 0 to 1, as said below
- factor_front: float32 [3, 12288, 512], P(None, 'row', 'col'), may hold values from -0.0546875 to 0.0546875
- factor_border: float32 [2, 512, 512], replicated, may hold values from -0.6 to 0.6
- pivot_inverse: float32 [3, 512, 512], P(None, 'row')
Outputs:
- inverse_front: float32 [3, 512, 12288], P(None, 'row', 'col')
- inverse_parent: float32 [2, 512, 512], P(None, 'row')
- inverse_diagonal: float32 [3, 512, 512], P(None, 'row')
Inputs may be any that keep to these rules, and one draw needn't show every extreme that they name: front is exactly symmetric. structure[k, b] = 1 where front block b (rows b * 128 to (b + 1) * 128 - 1) lies in supernode k's structure; every 1 in row k is also a 1 in row k - 1; blocks b < 24 are 1 in every row.
All inputs are finite; a program needn't handle non-finite values.
Results may differ from a plain program's by a relative error of at most 0.0001.
Values sent between devices are 32-bit elements; how exact they have to be, the bound alone decides.
No kernel may reach another device: no remote copies, remote signals or barrier semaphores. Data moves between devices by JAX's collectives and lax.ppermute only.
A program may use at most 128 MiB of HBM per device.

v0:
```python
import jax
import jax.numpy as jnp
from jax import lax
from jax.sharding import PartitionSpec as P

BLK = 128
HIGH = lax.Precision.HIGHEST


def broadcast(x, axis, root):
    mine = lax.axis_index(axis) == root
    return lax.psum(jnp.where(mine, x, jnp.zeros_like(x)), axis)


def matmul(former, latter):
    return jnp.dot(former, latter, precision=HIGH, preferred_element_type=jnp.float32)


def contract_first(former, latter):
    return lax.dot_general(
        former, latter, (((0,), (0,)), ((), ())), precision=HIGH, preferred_element_type=jnp.float32
    )


def block_flags(structure_row, first_row, rows_count):
    position = first_row + jnp.arange(rows_count, dtype=jnp.int32)
    owners = position // BLK
    numbers = jnp.arange(structure_row.shape[0], dtype=jnp.int32)
    matches = (owners[:, None] == numbers[None, :]).astype(jnp.float32)
    return jnp.dot(matches, structure_row.astype(jnp.float32), precision=HIGH)


def body(front, structure, factor_front, factor_border, pivot_inverse):
    row_index = lax.axis_index("row")
    col_index = lax.axis_index("col")
    rows_here = front.shape[0]
    cols_here = front.shape[1]
    width_here = pivot_inverse.shape[1]
    supers = structure.shape[0]
    row_first = row_index * rows_here
    col_first = col_index * cols_here
    fronts = []
    parents = []
    diagonals = []
    previous = None
    diag_prev = None
    for section in range(supers):
        gathered = lax.all_gather(factor_front[section], "col", axis=1, tiled=True)
        row_flags = block_flags(structure[section], row_first, rows_here)
        factor_rows = gathered * row_flags[:, None]
        own_half = lax.dynamic_slice_in_dim(factor_rows, col_index % 2 * cols_here, cols_here, 0)
        factor_cols = broadcast(own_half, "row", col_index // 2)
        partial_value = contract_first(factor_rows, front)
        if section > 0:
            border = factor_border[section - 1]
            border_rows = lax.dynamic_slice_in_dim(border, row_index * width_here, width_here, 0)
            partial_value = partial_value + contract_first(border_rows, previous)
            parent_part = lax.psum(matmul(previous, factor_cols), "col")
            parent_rows = parent_part + matmul(diag_prev, border)
            parent_all = lax.all_gather(parent_rows, "row", axis=0, tiled=True)
            parents.append(-parent_rows)
        image_rows = lax.psum_scatter(partial_value, "row", scatter_dimension=0, tiled=True)
        col_flags = block_flags(structure[section], col_first, cols_here)
        current = -(image_rows * col_flags[None, :])
        gram_rows = lax.psum(matmul(image_rows, factor_cols), "col")
        diag_now = pivot_inverse[section] + gram_rows
        if section > 0:
            parent_slice = lax.dynamic_slice_in_dim(
                parent_all, row_index * width_here, width_here, 1
            )
            diag_now = diag_now + contract_first(parent_slice, border)
        fronts.append(current)
        diagonals.append(diag_now)
        previous = current
        diag_prev = diag_now
    return (jnp.stack(fronts), jnp.stack(parents), jnp.stack(diagonals))


def solution(mesh):
    placed = (P("row", "col"), P(), P(None, "row", "col"), P(), P(None, "row", None))
    return jax.shard_map(
        body,
        mesh=mesh,
        in_specs=placed,
        out_specs=(P(None, "row", "col"), P(None, "row", None), P(None, "row", None)),
        check_vma=False,
    )
```

profile of v0, /device:TPU:0, one launch (start us, length us, event | category | flops | bytes accessed | tf_op | source)
XLA Modules:
  0.0 802.7 jit_solution(8092300581253794925)
XLA Ops:
  13.2 45.4 %all-gather.13.cloned.1.call-done = f32[1,3072,512]{1,2,0:T(8,128)} async-done(((f32[1,3072,64]{1,2,0:T(8,128)}), f32[1,3072,512]{1,2,0:T(8,128)}) %all-gather.13.cloned.1.call-update) | async-done | bytes 6291472 | tf_op jit(solution)/shard_map/all_gather | solution.py:48
  58.6 3.4 bitcast_multiply_fusion.2
  64.7 33.4 %fusion.63 = f32[512,1536]{1,0:T(8,128)} fusion(f32[3072,512]{0,1:T(8,128)S(1)} %bitcast_multiply_fusion.2, f32[3072,1536]{1,0:T(8,128)} %param.5), kind=kOutput, calls=%fused_computation.103 | convolution fusion | flops 28991029248 | bytes 28311552 | tf_op jit(solution)/shard_map/dot_general | solution.py:20
  105.9 3.4 bitcast_multiply_fusion.1
  111.9 33.4 %fusion.64 = f32[512,1536]{1,0:T(8,128)} fusion(f32[3072,512]{0,1:T(8,128)S(1)} %bitcast_multiply_fusion.1, f32[3072,1536]{1,0:T(8,128)} %param.5), kind=kOutput, calls=%fused_computation.104 | convolution fusion | flops 28991029248 | bytes 28311552 | tf_op jit(solution)/shard_map/dot_general | solution.py:20
  145.3 23.4 %reduce-scatter.4.cloned.1.call-done = f32[128,1536]{1,0:T(8,128)} async-done(((f32[512,1536]{1,0:T(8,128)}), f32[128,1536]{1,0:T(8,128)}) %reduce-scatter.4.cloned.1.call-update) | async-done | bytes 786448 | tf_op jit(solution)/shard_map/reduce_scatter | solution.py:62
  168.6 6.6 convolution_add_fusion.1
  177.5 4.1 dynamic-slice_select_fusion.2
  181.6 3.8 dynamic-slice_select_fusion.1
  185.4 30.3 %all-gather.17.cloned.1.call-done = f32[1,3072,512]{1,2,0:T(8,128)} async-done(((f32[1,3072,64]{1,2,0:T(8,128)}), f32[1,3072,512]{1,2,0:T(8,128)}) %all-gather.17.cloned.1.call-update) | async-done | bytes 6291472 | tf_op jit(solution)/shard_map/all_gather | solution.py:48
  215.7 3.4 bitcast_multiply_fusion
  224.4 35.4 %fusion.65 = f32[512,1536]{1,0:T(8,128)} fusion(f32[3072,512]{0,1:T(8,128)} %copy-done.3, f32[3072,1536]{1,0:T(8,128)} %param.5), kind=kOutput, calls=%fused_computation.105 | convolution fusion | flops 28991029248 | bytes 28311552 | tf_op jit(solution)/shard_map/dot_general | solution.py:20
  259.8 18.5 %reduce-scatter.6.cloned.1.call-done = f32[128,1536]{1,0:T(8,128)} async-done(((f32[512,1536]{1,0:T(8,128)}), f32[128,1536]{1,0:T(8,128)}) %reduce-scatter.6.cloned.1.call-update) | async-done | bytes 786448 | tf_op jit(solution)/shard_map/reduce_scatter | solution.py:62
  278.3 5.6 convolution_add_fusion
  284.2 321.4 %all-reduce.7.cloned.1.call-done = (f32[1536,512]{0,1:T(8,128)}, f32[1536,512]{0,1:T(8,128)}, f32[1536,512]{0,1:T(8,128)}) async-done(((f32[1536,512]{0,1:T(8,128)}, f32[1536,512]{0,1:T(8,128)}, f32[1536,512]{0,1:T(8,128)}), (f32[1536,512]{0,1:T(8,128)}, f32[1536,512]{0,1:T(8,128)}, f32[1536,512]{0,1:T(8,128)})) %all-reduce.7.cloned.1.call-update) | async-done | bytes 9437200 | tf_op jit(solution)/shard_map/psum | solution.py:12
  605.6 6.0 fusion.66
  611.6 3.9 fusion.11
  615.5 4.0 fusion.67
  619.6 3.9 fusion.13
  623.4 43.9 %reduce-scatter.8.cloned.1.call-done = f32[128,1536]{1,0:T(8,128)} async-done(((f32[512,1536]{1,0:T(8,128)}), f32[128,1536]{1,0:T(8,128)}) %reduce-scatter.8.cloned.1.call-update) | async-done | bytes 786448 | tf_op jit(solution)/shard_map/reduce_scatter | solution.py:62
  667.3 6.1 fusion.68
  673.8 58.5 %all-reduce.5.cloned.1.call-done = (f32[128,512]{1,0:T(8,128)}, f32[128,512]{1,0:T(8,128)}, f32[128,512]{1,0:T(8,128)}, f32[128,512]{1,0:T(8,128)}, f32[128,512]{1,0:T(8,128)}) async-done(((f32[128,512]{1,0:T(8,128)}, f32[128,512]{1,0:T(8,128)}, f32[128,512]{1,0:T(8,128)}, f32[128,512]{1,0:T(8,128)}, f32[128,512]{1,0:T(8,128)}), (f32[128,512]{1,0:T(8,128)}, f32[128,512]{1,0:T(8,128)}, f32[128,512]{1,0:T(8,128)}, ...) | async-done | bytes 1310736 | tf_op jit(solution)/shard_map/psum | solution.py:58
  738.7 23.4 %all-gather.9.cloned.1.call-done = f32[512,512]{1,0:T(8,128)} async-done(((f32[128,512]{1,0:T(8,128)}), f32[512,512]{1,0:T(8,128)}) %all-gather.9.cloned.1.call-update) | async-done | bytes 1048592 | tf_op jit(solution)/shard_map/all_gather | solution.py:60
  770.4 22.5 %all-gather.11.cloned.1.call-done = f32[512,512]{1,0:T(8,128)} async-done(((f32[128,512]{1,0:T(8,128)}), f32[512,512]{1,0:T(8,128)}) %all-gather.11.cloned.1.call-update) | async-done | bytes 1048592 | tf_op jit(solution)/shard_map/all_gather | solution.py:60
  (75 shorter events, 44.4 us)
Async XLA Ops:
  7.2 4.0 copy-start.14
  7.2 51.4 %all-gather.13.cloned.1.call-start = ((), (), s32[]{:S(2)}) async-start(), calls=%async_computation.8 | async-start | bytes 7077888 | tf_op jit(solution)/shard_map/all_gather | solution.py:48
  10.3 95.6 %all-gather.15.cloned.1.call-start = ((), (), s32[]{:S(2)}) async-start(), calls=%async_computation.9 | async-start | bytes 7077888 | tf_op jit(solution)/shard_map/all_gather | solution.py:48
  11.1 157.6 %reduce-scatter.4.cloned.1.call-start = ((), (), s32[]{:S(2)}) async-start(), calls=%async_computation.3 | async-start | bytes 3932160 | tf_op jit(solution)/shard_map/reduce_scatter | solution.py:62
  62.0 2.7 copy-start.1
  98.0 3.8 copy-start
  98.1 117.6 %all-gather.17.cloned.1.call-start = ((), (), s32[]{:S(2)}) async-start(), calls=%async_computation.10 | async-start | bytes 7077888 | tf_op jit(solution)/shard_map/all_gather | solution.py:48
  98.6 179.6 %reduce-scatter.6.cloned.1.call-start = ((), (), s32[]{:S(2)}) async-start(), calls=%async_computation.4 | async-start | bytes 3932160 | tf_op jit(solution)/shard_map/reduce_scatter | solution.py:62
  175.3 430.3 %all-reduce.7.cloned.1.call-start = ((), (), s32[]{:S(2)}) async-start(), calls=%async_computation.12 | async-start | bytes 18874368 | tf_op jit(solution)/shard_map/psum | solution.py:12
  219.1 2.7 copy-start.3
  223.7 443.5 %reduce-scatter.8.cloned.1.call-start = ((), (), s32[]{:S(2)}) async-start(), calls=%async_computation.5 | async-start | bytes 3932160 | tf_op jit(solution)/shard_map/reduce_scatter | solution.py:62
  283.9 321.7 %copy-start.4 = (f32[128,1536]{1,0:T(8,128)S(1)}, f32[128,1536]{1,0:T(8,128)}, u32[]{:S(2)}) copy-start(f32[128,1536]{1,0:T(8,128)} %reduce-scatter.4.cloned.1.call-done) | copy-start | bytes 2359300
  284.0 448.3 %all-reduce.5.cloned.1.call-start = ((), (), s32[]{:S(2)}) async-start(), calls=%async_computation.11 | async-start | bytes 2621440 | tf_op jit(solution)/shard_map/psum | solution.py:58
  605.6 6.0 copy-start.7
  611.6 3.9 copy-start.5
  615.5 4.0 copy-start.6
  673.5 88.6 %all-gather.9.cloned.1.call-start = ((), (), s32[]{:S(2)}) async-start(), calls=%async_computation.6 | async-start | bytes 1310720 | tf_op jit(solution)/shard_map/all_gather | solution.py:60
  734.8 29.1 %copy-start.13 = (f32[128,512]{1,0:T(8,128)S(1)}, f32[128,512]{1,0:T(8,128)}, u32[]{:S(2)}) copy-start(f32[128,512]{1,0:T(8,128)} %get-tuple-element.3) | copy-start | bytes 786436
  734.8 58.1 %all-gather.11.cloned.1.call-start = ((), (), s32[]{:S(2)}) async-start(), calls=%async_computation.7 | async-start | bytes 1310720 | tf_op jit(solution)/shard_map/all_gather | solution.py:60
  736.5 28.9 %copy-start.8 = (f32[128,1536]{1,0:T(8,128)S(1)}, f32[128,1536]{1,0:T(8,128)}, u32[]{:S(2)}) copy-start(f32[128,1536]{1,0:T(8,128)} %reduce-scatter.8.cloned.1.call-done) | copy-start | bytes 2359300
  765.4 3.1 copy-start.10
  765.4 3.1 copy-start.11
  765.5 4.0 copy-start.9
  765.5 27.4 %copy-start.12 = (f32[128,512]{1,0:T(8,128)S(1)}, f32[128,512]{1,0:T(8,128)}, u32[]{:S(2)}) copy-start(f32[128,512]{1,0:T(8,128)} %get-tuple-element.7) | copy-start | bytes 786436
  (1 other events, 2.6 us)
Sparse Core Ops, SparseCore 0:
  10.5 48.1 all-gather.12
  60.5 45.3 all-gather.14
  108.2 60.3 reduce-scatter.3
  170.4 45.2 all-gather.16
  217.9 60.3 reduce-scatter.5
  281.0 324.5 all-reduce.6
  607.9 59.3 reduce-scatter.7
  673.6 58.6 all-reduce.4
  735.0 27.0 all-gather.8
  765.5 27.3 all-gather.10
where the time goes:
time: 809 us; the launch traced here: 803 us
  waiting for transfers between devices  591 us (73%)
  matrix products  154 us (19%)
  other arithmetic  29 us (4%)
  between operations  14.7 us (2%)
  local copies, waits for them, and re-layouts  12.1 us (1%)
    psum x1, waiting for transfers between devices, broadcast(): return lax.psum(jnp.where(mine, x, jnp.zeros_like(x)), axis)  321 us
    dot_general x7, matrix products, contract_first(): lax.dot_general(former, latter, (((0,), (0,)), ((), ())), precision=HIGH,...  118 us
    reduce_scatter x3, waiting for transfers between devices, body(): lax.psum_scatter(partial_value, 'row', scatter_dimension=0, tiled=True)  85.7 us
    all_gather x3, waiting for transfers between devices, body(): gathered = lax.all_gather(factor_front[section], 'col', axis=1, tiled=True)  78.7 us
    psum x1, waiting for transfers between devices, body(): parent_part = lax.psum(matmul(previous, factor_cols), 'col')  58.5 us
    all_gather x2, waiting for transfers between devices, body(): parent_all = lax.all_gather(parent_rows, 'row', axis=0, tiled=True)  45.9 us
    dot_general x7, matrix products, matmul(): jnp.dot(former, latter, precision=HIGH, preferred_element_type=jnp.float32)  27.9 us
  transfers between devices with their start and end apart: 10, of which 10 were waited for; matrix products, arithmetic and copies ran while one was open for 21% of the time, Pallas kernels for 0%

commit v1 on v0

--- a/solution.py
+++ b/solution.py
@@ -2,6 +2,7 @@
 import jax.numpy as jnp
 from jax import lax
 from jax.sharding import PartitionSpec as P
+from jax.lax import all_gather
 
 BLK = 128
 HIGH = lax.Precision.HIGHEST
@@ -45,7 +46,13 @@
     previous = None
     diag_prev = None
     for section in range(supers):
-        gathered = lax.all_gather(factor_front[section], "col", axis=1, tiled=True)
+
+        def copies_carry(x0):
+            prior = all_gather(x0, axis_name="col")
+            tall = jnp.concatenate(prior, axis=1)
+            return tall
+
+        gathered = copies_carry(factor_front[section])
         row_flags = block_flags(structure[section], row_first, rows_here)
         factor_rows = gathered * row_flags[:, None]
         own_half = lax.dynamic_slice_in_dim(factor_rows, col_index % 2 * cols_here, cols_here, 0)

time: 809 us -> 809 us (level)
  no operation moved by 1% of the time
where the time goes in v1:
time: 809 us; the launch traced here: 803 us
  waiting for transfers between devices  591 us (73%)
  matrix products  154 us (19%)
  other arithmetic  29 us (4%)
  between operations  14.7 us (2%)
  local copies, waits for them, and re-layouts  12.1 us (1%)
    psum x1, waiting for transfers between devices, broadcast(): return lax.psum(jnp.where(mine, x, jnp.zeros_like(x)), axis)  321 us
    dot_general x7, matrix products, contract_first(): lax.dot_general(former, latter, (((0,), (0,)), ((), ())), precision=HIGH,...  118 us
    reduce_scatter x3, waiting for transfers between devices, body(): lax.psum_scatter(partial_value, 'row', scatter_dimension=0, tiled=True)  85.7 us
    all_gather x3, waiting for transfers between devices, copies_carry(): prior = all_gather(x0, axis_name='col')  78.7 us
    psum x1, waiting for transfers between devices, body(): parent_part = lax.psum(matmul(previous, factor_cols), 'col')  58.5 us
    all_gather x2, waiting for transfers between devices, body(): parent_all = lax.all_gather(parent_rows, 'row', axis=0, tiled=True)  45.9 us
    dot_general x7, matrix products, matmul(): jnp.dot(former, latter, precision=HIGH, preferred_element_type=jnp.float32)  27.9 us
  transfers between devices with their start and end apart: 10, of which 10 were waited for; matrix products, arithmetic and copies ran while one was open for 21% of the time, Pallas kernels for 0%

profile of v1, /device:TPU:0, one launch (start us, length us, event | category | flops | bytes accessed | tf_op | source)
XLA Modules:
  0.0 802.7 jit_solution(8092300581253794925)
XLA Ops:
  13.2 45.4 %all-gather.6.cloned.1.call-done = f32[8,3072,64]{1,2,0:T(8,128)} async-done(((f32[1,3072,64]{1,2,0:T(8,128)}), f32[8,3072,64]{1,2,0:T(8,128)}) %all-gather.6.cloned.1.call-update) | async-done | bytes 6291472 | tf_op jit(solution)/shard_map/all_gather | solution.py:51
  58.6 3.4 bitcast_multiply_fusion.2
  64.7 33.4 %fusion.63 = f32[512,1536]{1,0:T(8,128)} fusion(f32[3072,512]{0,1:T(8,128)S(1)} %bitcast_multiply_fusion.2, f32[3072,1536]{1,0:T(8,128)} %param.5), kind=kOutput, calls=%fused_computation.103 | convolution fusion | flops 28991029248 | bytes 28311552 | tf_op jit(solution)/shard_map/dot_general | solution.py:21
  105.9 3.4 bitcast_multiply_fusion.1
  111.9 33.4 %fusion.64 = f32[512,1536]{1,0:T(8,128)} fusion(f32[3072,512]{0,1:T(8,128)S(1)} %bitcast_multiply_fusion.1, f32[3072,1536]{1,0:T(8,128)} %param.5), kind=kOutput, calls=%fused_computation.104 | convolution fusion | flops 28991029248 | bytes 28311552 | tf_op jit(solution)/shard_map/dot_general | solution.py:21
  145.3 23.4 %reduce-scatter.4.cloned.1.call-done = f32[128,1536]{1,0:T(8,128)} async-done(((f32[512,1536]{1,0:T(8,128)}), f32[128,1536]{1,0:T(8,128)}) %reduce-scatter.4.cloned.1.call-update) | async-done | bytes 786448 | tf_op jit(solution)/shard_map/reduce_scatter | solution.py:69
  168.6 6.6 convolution_add_fusion.1
  177.5 4.1 dynamic-slice_select_fusion.2
  181.6 3.8 dynamic-slice_select_fusion.1
  185.4 30.3 %all-gather.10.cloned.1.call-done = f32[8,3072,64]{1,2,0:T(8,128)} async-done(((f32[1,3072,64]{1,2,0:T(8,128)}), f32[8,3072,64]{1,2,0:T(8,128)}) %all-gather.10.cloned.1.call-update) | async-done | bytes 6291472 | tf_op jit(solution)/shard_map/all_gather | solution.py:51
  215.7 3.4 bitcast_multiply_fusion
  224.4 35.4 %fusion.65 = f32[512,1536]{1,0:T(8,128)} fusion(f32[3072,512]{0,1:T(8,128)} %copy-done.3, f32[3072,1536]{1,0:T(8,128)} %param.5), kind=kOutput, calls=%fused_computation.105 | convolution fusion | flops 28991029248 | bytes 28311552 | tf_op jit(solution)/shard_map/dot_general | solution.py:21
  259.8 18.5 %reduce-scatter.6.cloned.1.call-done = f32[128,1536]{1,0:T(8,128)} async-done(((f32[512,1536]{1,0:T(8,128)}), f32[128,1536]{1,0:T(8,128)}) %reduce-scatter.6.cloned.1.call-update) | async-done | bytes 786448 | tf_op jit(solution)/shard_map/reduce_scatter | solution.py:69
  278.3 5.6 convolution_add_fusion
  284.2 321.4 %all-reduce.7.cloned.1.call-done = (f32[1536,512]{0,1:T(8,128)}, f32[1536,512]{0,1:T(8,128)}, f32[1536,512]{0,1:T(8,128)}) async-done(((f32[1536,512]{0,1:T(8,128)}, f32[1536,512]{0,1:T(8,128)}, f32[1536,512]{0,1:T(8,128)}), (f32[1536,512]{0,1:T(8,128)}, f32[1536,512]{0,1:T(8,128)}, f32[1536,512]{0,1:T(8,128)})) %all-reduce.7.cloned.1.call-update) | async-done | bytes 9437200 | tf_op jit(solution)/shard_map/psum | solution.py:13
  605.6 6.0 fusion.66
  611.6 3.9 fusion.11
  615.5 4.0 fusion.67
  619.6 3.9 fusion.13
  623.4 43.9 %reduce-scatter.8.cloned.1.call-done = f32[128,1536]{1,0:T(8,128)} async-done(((f32[512,1536]{1,0:T(8,128)}), f32[128,1536]{1,0:T(8,128)}) %reduce-scatter.8.cloned.1.call-update) | async-done | bytes 786448 | tf_op jit(solution)/shard_map/reduce_scatter | solution.py:69
  667.3 6.1 fusion.68
  673.8 58.5 %all-reduce.5.cloned.1.call-done = (f32[128,512]{1,0:T(8,128)}, f32[128,512]{1,0:T(8,128)}, f32[128,512]{1,0:T(8,128)}, f32[128,512]{1,0:T(8,128)}, f32[128,512]{1,0:T(8,128)}) async-done(((f32[128,512]{1,0:T(8,128)}, f32[128,512]{1,0:T(8,128)}, f32[128,512]{1,0:T(8,128)}, f32[128,512]{1,0:T(8,128)}, f32[128,512]{1,0:T(8,128)}), (f32[128,512]{1,0:T(8,128)}, f32[128,512]{1,0:T(8,128)}, f32[128,512]{1,0:T(8,128)}, ...) | async-done | bytes 1310736 | tf_op jit(solution)/shard_map/psum | solution.py:65
  738.7 23.4 %all-gather.12.cloned.1.call-done = f32[512,512]{1,0:T(8,128)} async-done(((f32[128,512]{1,0:T(8,128)}), f32[512,512]{1,0:T(8,128)}) %all-gather.12.cloned.1.call-update) | async-done | bytes 1048592 | tf_op jit(solution)/shard_map/all_gather | solution.py:67
  770.4 22.5 %all-gather.14.cloned.1.call-done = f32[512,512]{1,0:T(8,128)} async-done(((f32[128,512]{1,0:T(8,128)}), f32[512,512]{1,0:T(8,128)}) %all-gather.14.cloned.1.call-update) | async-done | bytes 1048592 | tf_op jit(solution)/shard_map/all_gather | solution.py:67
  (75 shorter events, 44.4 us)
Async XLA Ops:
  7.2 4.0 copy-start.14
  7.2 51.4 %all-gather.6.cloned.1.call-start = ((), (), s32[]{:S(2)}) async-start(), calls=%async_computation.3 | async-start | bytes 7077888 | tf_op jit(solution)/shard_map/all_gather | solution.py:51
  10.3 95.6 %all-gather.8.cloned.1.call-start = ((), (), s32[]{:S(2)}) async-start(), calls=%async_computation.5 | async-start | bytes 7077888 | tf_op jit(solution)/shard_map/all_gather | solution.py:51
  11.1 157.6 %reduce-scatter.4.cloned.1.call-start = ((), (), s32[]{:S(2)}) async-start(), calls=%async_computation.4 | async-start | bytes 3932160 | tf_op jit(solution)/shard_map/reduce_scatter | solution.py:69
  62.0 2.7 copy-start.1
  98.0 3.8 copy-start
  98.1 117.6 %all-gather.10.cloned.1.call-start = ((), (), s32[]{:S(2)}) async-start(), calls=%async_computation.7 | async-start | bytes 7077888 | tf_op jit(solution)/shard_map/all_gather | solution.py:51
  98.6 179.6 %reduce-scatter.6.cloned.1.call-start = ((), (), s32[]{:S(2)}) async-start(), calls=%async_computation.6 | async-start | bytes 3932160 | tf_op jit(solution)/shard_map/reduce_scatter | solution.py:69
  175.3 430.3 %all-reduce.7.cloned.1.call-start = ((), (), s32[]{:S(2)}) async-start(), calls=%async_computation.12 | async-start | bytes 18874368 | tf_op jit(solution)/shard_map/psum | solution.py:13
  219.1 2.7 copy-start.3
  223.7 443.5 %reduce-scatter.8.cloned.1.call-start = ((), (), s32[]{:S(2)}) async-start(), calls=%async_computation.8 | async-start | bytes 3932160 | tf_op jit(solution)/shard_map/reduce_scatter | solution.py:69
  283.9 321.7 %copy-start.4 = (f32[128,1536]{1,0:T(8,128)S(1)}, f32[128,1536]{1,0:T(8,128)}, u32[]{:S(2)}) copy-start(f32[128,1536]{1,0:T(8,128)} %reduce-scatter.4.cloned.1.call-done) | copy-start | bytes 2359300
  284.0 448.3 %all-reduce.5.cloned.1.call-start = ((), (), s32[]{:S(2)}) async-start(), calls=%async_computation.11 | async-start | bytes 2621440 | tf_op jit(solution)/shard_map/psum | solution.py:65
  605.6 6.0 copy-start.7
  611.6 3.9 copy-start.5
  615.5 4.0 copy-start.6
  673.5 88.6 %all-gather.12.cloned.1.call-start = ((), (), s32[]{:S(2)}) async-start(), calls=%async_computation.9 | async-start | bytes 1310720 | tf_op jit(solution)/shard_map/all_gather | solution.py:67
  734.8 29.1 %copy-start.13 = (f32[128,512]{1,0:T(8,128)S(1)}, f32[128,512]{1,0:T(8,128)}, u32[]{:S(2)}) copy-start(f32[128,512]{1,0:T(8,128)} %get-tuple-element.3) | copy-start | bytes 786436
  734.8 58.1 %all-gather.14.cloned.1.call-start = ((), (), s32[]{:S(2)}) async-start(), calls=%async_computation.10 | async-start | bytes 1310720 | tf_op jit(solution)/shard_map/all_gather | solution.py:67
  736.5 28.9 %copy-start.8 = (f32[128,1536]{1,0:T(8,128)S(1)}, f32[128,1536]{1,0:T(8,128)}, u32[]{:S(2)}) copy-start(f32[128,1536]{1,0:T(8,128)} %reduce-scatter.8.cloned.1.call-done) | copy-start | bytes 2359300
  765.4 3.1 copy-start.10
  765.4 3.1 copy-start.11
  765.5 4.0 copy-start.9
  765.5 27.4 %copy-start.12 = (f32[128,512]{1,0:T(8,128)S(1)}, f32[128,512]{1,0:T(8,128)}, u32[]{:S(2)}) copy-start(f32[128,512]{1,0:T(8,128)} %get-tuple-element.7) | copy-start | bytes 786436
  (1 other events, 2.6 us)
Sparse Core Ops, SparseCore 0:
  10.5 48.1 all-gather.5
  60.5 45.3 all-gather.7
  108.2 60.3 reduce-scatter.3
  170.4 45.2 all-gather.9
  217.9 60.3 reduce-scatter.5
  281.0 324.5 all-reduce.6
  607.9 59.3 reduce-scatter.7
  673.6 58.6 all-reduce.4
  735.0 27.0 all-gather.11
  765.5 27.3 all-gather.13
